TPU v7x, 256 devices: a whole 4x4x8 slice. The times are simulated.
256 devices in a mesh: layer: 4 (over y_hi, core), latent: 64 (over x, z, y_lo).
Axes of the slice: x: 4, y: 4 (y_hi: 2, y_lo: 2; y = y_hi * 2 + y_lo), z: 8, core: 2. Of those that a mesh axis runs over, the one named last changes fastest.
Arguments:
- inputs: bfloat16 [4, 128, 4096], P('layer', 'latent'), may hold values from -6 to 6
- targets: bfloat16 [4, 128, 4096], P('layer', 'latent'), may hold values from -6 to 6
- w_enc: bfloat16 [4, 4096, 8192], P('layer', None, 'latent'), may hold values from -0.09375 to 0.09375
- b_enc: float32 [4, 8192], P('layer', 'latent'), may hold values from -3 to 3
- w_dec: bfloat16 [4, 4, 8192, 4096], P('layer', None, 'latent'), may hold values from -0.03125 to 0.03125
- b_dec: float32 [4, 4096], P('layer'), may hold values from -3 to 3
Outputs:
- grad_enc: bfloat16 [4, 4096, 8192], P('layer', None, 'latent')
- grad_benc: float32 [4, 8192], P('layer', 'latent')
- grad_dec: bfloat16 [4, 4, 8192, 4096], P('layer', None, 'latent')
- grad_bdec: float32 [4, 4096], P('layer')
All inputs are finite; a program needn't handle non-finite values.
Results may differ from a plain program's by a relative error of at most 0.0057.
Values may be sent and summed in bfloat16 or wider, within the bound.
No kernel may reach another device: no remote copies, remote signals or barrier semaphores. Data moves between devices by JAX's collectives and lax.ppermute only.
A program may use at most 64 MiB of HBM per device.

v0:
```python
import jax
import jax.numpy as jnp
from jax import lax
from jax.sharding import PartitionSpec as P

penalty = 0.5
eps = 1e-06


def sent_to_all(x, axis):
    copies = jnp.broadcast_to(x, (lax.axis_size(axis), *x.shape))
    return lax.all_to_all(copies, axis, split_axis=0, concat_axis=0, tiled=True)


def in_order(pieces, dim):
    pieces = jnp.moveaxis(pieces, 0, dim)
    lengths = pieces.shape
    return pieces.reshape(*lengths[:dim], lengths[dim] * lengths[dim + 1], *lengths[dim + 2 :])


def gather_directly(x, axis, dim):
    pieces = sent_to_all(x, axis)
    return in_order(pieces, dim)


def cut_along(x, dim, length):
    lengths = x.shape
    pieces = x.reshape(*lengths[:dim], length, lengths[dim] // length, *lengths[dim + 1 :])
    return jnp.moveaxis(pieces, dim, 0)


def summed_on_arrival(x, axis, dim):
    length = lax.axis_size(axis)
    pieces = lax.all_to_all(cut_along(x, dim, length), axis, 0, 0, tiled=True)
    return jnp.sum(pieces, axis=0)


def taken_together(x, axis):
    return sent_to_all(x, axis).sum(axis=0)


def local(inputs, targets, w_enc, b_enc, w_dec, b_dec):
    source = lax.axis_index("layer")
    depth = w_dec.shape[1]
    whole = gather_directly(inputs[0], "latent", 0)
    pre = jnp.dot(whole, w_enc[0], preferred_element_type=jnp.float32) + b_enc[0]
    positive = jnp.maximum(pre, 0.0)
    act = (positive * positive).astype(jnp.bfloat16)
    valid = (jnp.arange(depth, dtype=jnp.int32) >= source).astype(jnp.float32)
    partial_value = (
        jnp.einsum("nk,tkd->tnd", act, w_dec[0], preferred_element_type=jnp.float32)
        * valid[:, None, None]
    )
    spread = lax.psum_scatter(partial_value, "layer", scatter_dimension=0, tiled=True)
    recon = summed_on_arrival(spread, "latent", 1)
    error = recon[0] + b_dec[0] - targets[0].astype(jnp.float32)
    grad_bdec = taken_together(jnp.sum(error, axis=0), "latent")[None, :]
    err_low = error.astype(jnp.bfloat16)[None]
    stacked = gather_directly(err_low, "latent", 1)
    errors = lax.all_gather(stacked, "layer", axis=0, tiled=True)
    errors = jnp.where(valid[:, None, None] > 0.0, errors, jnp.zeros_like(errors))
    decoders = w_dec[0]
    squares = jnp.sum(jnp.square(decoders.astype(jnp.float32)), axis=2)
    norms = jnp.sqrt(jnp.sum(squares * valid[:, None], axis=0) + eps)
    back = jnp.einsum("tnd,tkd->nk", errors, decoders, preferred_element_type=jnp.float32)
    d_act = back + penalty * norms[None, :]
    d_pre = d_act * 2.0 * positive
    grad_benc = jnp.sum(d_pre, axis=0)[None, :]
    d_low = d_pre.astype(jnp.bfloat16)
    grad_enc = lax.dot_general(
        whole, d_low, (((0,), (0,)), ((), ())), preferred_element_type=jnp.float32
    ).astype(jnp.bfloat16)[None]
    act_total = jnp.sum(act.astype(jnp.float32), axis=0)
    scale = penalty * act_total / norms
    grad_mse = jnp.einsum("nk,tnd->tkd", act, errors, preferred_element_type=jnp.float32)
    shrink = valid[:, None, None] * scale[None, :, None] * decoders.astype(jnp.float32)
    grad_dec = (grad_mse + shrink).astype(jnp.bfloat16)[None]
    return (grad_enc, grad_benc, grad_dec, grad_bdec)


def solution(mesh):
    placed = (
        P("layer", "latent", None),
        P("layer", "latent", None),
        P("layer", None, "latent"),
        P("layer", "latent"),
        P("layer", None, "latent", None),
        P("layer", None),
    )
    return jax.shard_map(
        local,
        mesh=mesh,
        in_specs=placed,
        out_specs=(
            P("layer", None, "latent"),
            P("layer", "latent"),
            P("layer", None, "latent", None),
            P("layer", None),
        ),
        check_vma=False,
    )
```

profile of v0, /device:TPU:1, one launch (start us, length us, event | category | flops | bytes accessed | tf_op | source)
XLA Modules:
  0.0 318.3 jit_solution(515087838931278608)
XLA Ops:
  7.2 0.0 copy-start
  7.2 0.0 copy-start.3
  7.2 2.8 broadcast_in_dim.40
  10.0 13.5 %all-to-all-start = ((bf16[64,2,4096]{2,1,0:T(2,128)(2,1)}), bf16[64,2,4096]{2,1,0:T(2,128)(2,1)S(1)}, u32[]{:S(2)}, u32[]{:S(2)}) async-start(bf16[64,2,4096]{2,1,0:T(2,128)(2,1)} %broadcast_in_dim.40), calls=%async_computation | async-start | bytes 2097152 | tf_op jit(solution)/shard_map/all_to_all | solution.py:12
  23.5 0.0 reduce-scatter.2.cloned.1.call-start
  23.5 27.1 %all-to-all-done = bf16[64,2,4096]{2,1,0:T(2,128)(2,1)S(1)} async-done(((bf16[64,2,4096]{2,1,0:T(2,128)(2,1)}), bf16[64,2,4096]{2,1,0:T(2,128)(2,1)S(1)}, u32[]{:S(2)}, u32[]{:S(2)}) %all-to-all-start) | async-done | bytes 1048608 | tf_op jit(solution)/shard_map/all_to_all | solution.py:12
  50.6 0.4 reshape.76
  51.1 0.0 copy-done
  51.1 0.0 copy-done.3
  51.1 0.4 convert_reduce_fusion
  51.5 6.7 %multiply_bitcast_fusion = f32[4,128,4096]{2,1,0:T(8,128)} fusion(bf16[1,4,128,4096]{3,2,1,0:T(8,128)(2,1)} %param.10, f32[4]{0:T(128)S(1)} %compare_convert_fusion, f32[128,128]{1,0:T(8,128)S(1)} %get-tuple-element.29), kind=kOutput, calls=%fused_computation.5 | convolution fusion | flops 539000832 | bytes 12648464 | tf_op jit(solution)/shard_map/nk,tkd->tnd/dot_general | solution.py:51
  58.2 0.0 reduce-scatter.2.cloned.1.call-update
  58.2 0.0 all-gather.2.cloned.1.call-start
  58.3 81.5 %reduce-scatter.2.cloned.1.call-done = f32[1,128,4096]{2,1,0:T(8,128)} async-done(((f32[4,128,4096]{2,1,0:T(8,128)}), f32[1,128,4096]{2,1,0:T(8,128)}) %reduce-scatter.2.cloned.1.call-update) | async-done | bytes 2097168 | tf_op jit(solution)/shard_map/reduce_scatter | solution.py:54
  139.8 3.4 %transpose_reshape.3 = f32[64,1,2,4096]{3,2,0,1:T(2,128)} reshape(f32[1,128,4096]{2,1,0:T(8,128)} %reduce-scatter.2.cloned.1.call-done) | data formatting | bytes 4194304 | tf_op jit(solution)/shard_map/transpose;reshape | solution.py:29
  143.2 0.0 copy-start.1
  143.2 0.0 copy-start.2
  143.2 59.8 %all_to_all.21 = f32[64,1,2,4096]{3,2,1,0:T(2,128)} all-to-all(f32[64,1,2,4096]{3,2,1,0:T(2,128)} %bitcast.65), channel_id=1, replica_groups=mesh['layer'=4,'latent'=64] {'latent'}, dimensions={0} | all-to-all | bytes 4194304 | tf_op jit(solution)/shard_map/all_to_all | solution.py:34
  203.0 2.2 reduce_sum.63
  205.3 0.0 copy-done.1
  205.3 0.0 copy-done.2
  205.3 0.1 fusion.25
  205.4 1.0 broadcast_in_dim.41
  206.4 33.9 %all_to_all.22 = bf16[64,1,2,4096]{3,2,1,0:T(2,128)(2,1)S(1)} all-to-all(bf16[64,1,2,4096]{3,2,1,0:T(2,128)(2,1)S(1)} %broadcast_in_dim.41), channel_id=1, replica_groups=mesh['layer'=4,'latent'=64] {'latent'}, dimensions={0} | all-to-all | bytes 2097152 | tf_op jit(solution)/shard_map/all_to_all | solution.py:12
  240.3 1.2 reshape_transpose.3
  241.5 0.0 all-gather.2.cloned.1.call-update
  241.5 2.0 broadcast_in_dim.46
  243.5 7.5 %all-to-all-start.3 = ((f32[64,1,4096]{2,1,0:T(1,128)}), f32[64,1,4096]{2,1,0:T(1,128)S(1)}, u32[]{:S(2)}, u32[]{:S(2)}) async-start(f32[64,1,4096]{2,1,0:T(1,128)} %broadcast_in_dim.46), calls=%async_computation.4 | async-start | bytes 2097152 | tf_op jit(solution)/shard_map/all_to_all | solution.py:12
  251.0 6.5 %copy.37 = bf16[1,4,128,4096]{2,3,1,0:T(8,128)(2,1)} copy(bf16[1,4,128,4096]{3,2,1,0:T(8,128)(2,1)} %param.10) | data formatting | bytes 8388608 | tf_op args[4]
  257.5 3.0 fusion
  260.5 0.1 multiply_reduce_fusion
  260.6 0.1 broadcast_multiply_fusion
  260.7 17.0 %all-to-all-done.3 = f32[64,1,4096]{2,1,0:T(1,128)S(1)} async-done(((f32[64,1,4096]{2,1,0:T(1,128)}), f32[64,1,4096]{2,1,0:T(1,128)S(1)}, u32[]{:S(2)}, u32[]{:S(2)}) %all-to-all-start.3) | async-done | bytes 1048608 | tf_op jit(solution)/shard_map/all_to_all | solution.py:12
  277.7 1.6 reduce_sum.69
  279.2 11.7 %all-gather.2.cloned.1.call-done = bf16[4,128,4096]{2,1,0:T(8,128)(2,1)} async-done(((bf16[1,128,4096]{2,1,0:T(8,128)(2,1)}), bf16[4,128,4096]{2,1,0:T(8,128)(2,1)}) %all-gather.2.cloned.1.call-update) | async-done | bytes 4194320 | tf_op jit(solution)/shard_map/all_gather | solution.py:60
  291.0 5.3 %fusion.29 = (f32[128]{0:T(128)}, bf16[128,128]{1,0:T(8,128)(2,1)S(1)}) fusion(f32[128,128]{1,0:T(8,128)S(1)} %get-tuple-element.29, f32[128]{0:T(128)S(1)} %get-tuple-element.27, bf16[1,4,128,4096]{3,2,1,0:T(8,128)(2,1)} %param.10, bf16[4,128,4096]{2,1,0:T(8,128)(2,1)} %all-gather.2.cloned.1.call-done, pred[4]{0:T(512)(128)(4,1)S(1)} %broadcast_compare_fusion), kind=kOutput, calls=%fused_computation.36 | convolution fusion | flops 539049856 | bytes 8487940 | tf_op jit(solution)/shard_map/tnd,tkd->nk/dot_general | solution.py:65
  296.3 0.5 fusion.4
  296.7 1.3 copy.43
  298.1 7.1 %fusion.3 = bf16[1,4,128,4096]{2,3,1,0:T(8,128)(2,1)} fusion(bf16[1,4,128,4096]{2,3,1,0:T(8,128)(2,1)} %copy.37, f32[4,128]{1,0:T(4,128)S(1)} %broadcast_multiply_fusion, bf16[4,128,4096]{2,1,0:T(8,128)(2,1)} %all-gather.2.cloned.1.call-done, pred[4]{0:T(512)(128)(4,1)S(1)} %broadcast_compare_fusion, f32[128,128]{1,0:T(8,128)S(1)} %get-tuple-element.29), kind=kOutput, calls=%fused_computation.6 | convolution fusion | flops 547389440 | bytes 12650500 | tf_op jit(solution)/shard_map/nk,tnd->tkd/dot_general | solution.py:75
  305.2 6.3 %copy.44 = bf16[1,4,128,4096]{3,2,1,0:T(8,128)(2,1)} copy(bf16[1,4,128,4096]{2,3,1,0:T(8,128)(2,1)} %fusion.3) | data formatting | bytes 8388608
  (3 shorter events, 0.0 us)
Async XLA Ops:
  7.2 43.9 %copy-start = (bf16[1,4096,128]{2,1,0:T(8,128)(2,1)S(1)}, bf16[1,4096,128]{2,1,0:T(8,128)(2,1)}, u32[]{:S(2)}) copy-start(bf16[1,4096,128]{2,1,0:T(8,128)(2,1)} %param.8) | copy-start | bytes 3145732
  7.2 43.9 %copy-start.3 = (f32[1,128]{1,0:T(1,128)S(1)}, f32[1,128]{1,0:T(1,128)}, u32[]{:S(2)}) copy-start(f32[1,128]{1,0:T(1,128)} %param.9) | copy-start | bytes 1540
  10.0 40.7 %all-to-all-start = ((bf16[64,2,4096]{2,1,0:T(2,128)(2,1)}), bf16[64,2,4096]{2,1,0:T(2,128)(2,1)S(1)}, u32[]{:S(2)}, u32[]{:S(2)}) async-start(bf16[64,2,4096]{2,1,0:T(2,128)(2,1)} %broadcast_in_dim.40), calls=%async_computation | async-start | bytes 2097152 | tf_op jit(solution)/shard_map/all_to_all | solution.py:12
  23.5 116.3 %reduce-scatter.2.cloned.1.call-start = ((), (), s32[]{:S(2)}) async-start(), calls=%async_computation.5 | async-start | bytes 10485760 | tf_op jit(solution)/shard_map/reduce_scatter | solution.py:54
  58.2 232.8 %all-gather.2.cloned.1.call-start = ((), (), s32[]{:S(2)}) async-start(), calls=%async_computation.6 | async-start | bytes 5242880 | tf_op jit(solution)/shard_map/all_gather | solution.py:60
  143.2 62.1 %copy-start.1 = (bf16[1,2,4096]{2,1,0:T(2,128)(2,1)S(1)}, bf16[1,2,4096]{2,1,0:T(2,128)(2,1)}, u32[]{:S(2)}) copy-start(bf16[1,2,4096]{2,1,0:T(2,128)(2,1)} %param.7) | copy-start | bytes 49156
  143.2 62.1 %copy-start.2 = (f32[1,4096]{1,0:T(1,128)S(1)}, f32[1,4096]{1,0:T(1,128)}, u32[]{:S(2)}) copy-start(f32[1,4096]{1,0:T(1,128)} %param.11) | copy-start | bytes 49156
  243.5 34.2 %all-to-all-start.3 = ((f32[64,1,4096]{2,1,0:T(1,128)}), f32[64,1,4096]{2,1,0:T(1,128)S(1)}, u32[]{:S(2)}, u32[]{:S(2)}) async-start(f32[64,1,4096]{2,1,0:T(1,128)} %broadcast_in_dim.46), calls=%async_computation.4 | async-start | bytes 2097152 | tf_op jit(solution)/shard_map/all_to_all | solution.py:12
Sparse Core Ops, SparseCore 0:
  58.3 81.3 reduce-scatter.1
  241.6 49.3 all-gather.1
where the time goes:
time: 319 us; the launch traced here: 318 us
  waiting for transfers between devices  137 us (43%)
  blocking collectives  93.7 us (29%)
  local copies, waits for them, and re-layouts  25 us (8%)
  starting transfers between devices  21.1 us (7%)
  matrix products  20 us (6%)
  between operations  14.2 us (4%)
  other arithmetic  7.06 us (2%)
    reduce_scatter x1, waiting for transfers between devices, local(): lax.psum_scatter(partial_value, 'layer', scatter_dimension=0, tiled=True)  81.5 us
    all_to_all x1, blocking collectives, summed_on_arrival(): pieces = lax.all_to_all(cut_along(x, dim, length), axis, 0, 0, tiled=True)  59.8 us
    all_to_all x2, waiting for transfers between devices, sent_to_all(): return lax.all_to_all(copies, axis, split_axis=0, concat_axis=0, tiled=True)  44.1 us
    all_to_all x1, blocking collectives, sent_to_all(): return lax.all_to_all(copies, axis, split_axis=0, concat_axis=0, tiled=True)  33.9 us
    all_to_all x2, starting transfers between devices, sent_to_all(): return lax.all_to_all(copies, axis, split_axis=0, concat_axis=0, tiled=True)  21 us
    unnamed x11, local copies, waits for them, and re-layouts  14.2 us
    all_gather x1, waiting for transfers between devices, local(): errors = lax.all_gather(stacked, 'layer', axis=0, tiled=True)  11.7 us
    dot_general x1, matrix products, local(): jnp.einsum('nk,tnd->tkd', act, errors, preferred_element_type=jnp.float32)  7.11 us
  transfers between devices with their start and end apart: 4, of which 4 were waited for; matrix products, arithmetic and copies ran while one was open for 4% of the time, Pallas kernels for 0%

commit v1 on v0

--- a/solution.py
+++ b/solution.py
@@ -1,3 +1,4 @@
+import functools
 import jax
 import jax.numpy as jnp
 from jax import lax
@@ -5,6 +6,15 @@
 
 penalty = 0.5
 eps = 1e-06
+
+
+def get_arrays(here_x, axis_key, d0):
+    long_array = jnp.stack(lax.axis_size(axis_key) * [here_x], 0)
+    new = lax.all_to_all(long_array, axis_name=axis_key, split_axis=0, concat_axis=0)
+    return jnp.concatenate(new, d0)
+
+
+unite_floor_all = functools.partial(get_arrays, axis_key="layer", d0=0)
 
 
 def sent_to_all(x, axis):
@@ -57,7 +67,7 @@
     grad_bdec = taken_together(jnp.sum(error, axis=0), "latent")[None, :]
     err_low = error.astype(jnp.bfloat16)[None]
     stacked = gather_directly(err_low, "latent", 1)
-    errors = lax.all_gather(stacked, "layer", axis=0, tiled=True)
+    errors = unite_floor_all(stacked)
     errors = jnp.where(valid[:, None, None] > 0.0, errors, jnp.zeros_like(errors))
     decoders = w_dec[0]
     squares = jnp.sum(jnp.square(decoders.astype(jnp.float32)), axis=2)

time: 319 us -> 364 us (1.14)
  waiting for transfers between devices: 137 us -> 169 us
  starting transfers between devices: 21.1 us -> 28.8 us
  local copies, waits for them, and re-layouts: 25 us -> 29 us
    all_to_all x0 -> x1, waiting for transfers between devices: none -> 36.6 us  [get_arrays(): lax.all_to_all(long_array, axis_name=axis_key, split_axis=0, concat_axis=0)]
    all_gather x1 -> x0, waiting for transfers between devices: 11.7 us -> none  [local(): errors = lax.all_gather(stacked, 'layer', axis=0, tiled=True)]
    all_to_all x0 -> x1, starting transfers between devices: none -> 7.75 us  [get_arrays(): lax.all_to_all(long_array, axis_name=axis_key, split_axis=0, concat_axis=0)]
    all_to_all x2, waiting for transfers between devices: 44.1 us -> 51 us  [sent_to_all(): return lax.all_to_all(copies, axis, split_axis=0, concat_axis=0, tiled=True)]
    another operation x1 -> x3, local copies, waits for them, and re-layouts: 1.2 us -> 5.34 us  [get_arrays(): long_array = jnp.stack(lax.axis_size(axis_key) * [here_x], 0)]
where the time goes in v1:
time: 364 us; the launch traced here: 363 us
  waiting for transfers between devices  169 us (46%)
  blocking collectives  93.7 us (26%)
  local copies, waits for them, and re-layouts  29 us (8%)
  starting transfers between devices  28.8 us (8%)
  matrix products  19.9 us (5%)
  between operations  14.2 us (4%)
  other arithmetic  8.17 us (2%)
    reduce_scatter x1, waiting for transfers between devices, local(): lax.psum_scatter(partial_value, 'layer', scatter_dimension=0, tiled=True)  81.5 us
    all_to_all x1, blocking collectives, summed_on_arrival(): pieces = lax.all_to_all(cut_along(x, dim, length), axis, 0, 0, tiled=True)  59.8 us
    all_to_all x2, waiting for transfers between devices, sent_to_all(): return lax.all_to_all(copies, axis, split_axis=0, concat_axis=0, tiled=True)  51 us
    all_to_all x1, waiting for transfers between devices, get_arrays(): lax.all_to_all(long_array, axis_name=axis_key, split_axis=0, concat_axis=0)  36.6 us
    all_to_all x1, blocking collectives, sent_to_all(): return lax.all_to_all(copies, axis, split_axis=0, concat_axis=0, tiled=True)  33.9 us
    all_to_all x2, starting transfers between devices, sent_to_all(): return lax.all_to_all(copies, axis, split_axis=0, concat_axis=0, tiled=True)  21.1 us
    unnamed x11, local copies, waits for them, and re-layouts  14 us
    all_to_all x1, starting transfers between devices, get_arrays(): lax.all_to_all(long_array, axis_name=axis_key, split_axis=0, concat_axis=0)  7.75 us
  transfers between devices with their start and end apart: 4, of which 4 were waited for; matrix products, arithmetic and copies ran while one was open for 4% of the time, Pallas kernels for 0%

profile of v1, /device:TPU:1, one launch (start us, length us, event | category | flops | bytes accessed | tf_op | source)
XLA Modules:
  0.0 362.9 jit_solution(492186709906087559)
XLA Ops:
  7.2 0.0 copy-start
  7.2 0.0 copy-start.3
  7.2 2.8 broadcast_in_dim.40
  10.0 13.5 %all-to-all-start = ((bf16[64,2,4096]{2,1,0:T(2,128)(2,1)}), bf16[64,2,4096]{2,1,0:T(2,128)(2,1)S(1)}, u32[]{:S(2)}, u32[]{:S(2)}) async-start(bf16[64,2,4096]{2,1,0:T(2,128)(2,1)} %broadcast_in_dim.40), calls=%async_computation | async-start | bytes 2097152 | tf_op jit(solution)/shard_map/all_to_all | solution.py:22
  23.5 0.0 reduce-scatter.2.cloned.1.call-start
  23.5 27.1 %all-to-all-done = bf16[64,2,4096]{2,1,0:T(2,128)(2,1)S(1)} async-done(((bf16[64,2,4096]{2,1,0:T(2,128)(2,1)}), bf16[64,2,4096]{2,1,0:T(2,128)(2,1)S(1)}, u32[]{:S(2)}, u32[]{:S(2)}) %all-to-all-start) | async-done | bytes 1048608 | tf_op jit(solution)/shard_map/all_to_all | solution.py:22
  50.6 0.4 reshape.83
  51.1 0.0 copy-done
  51.1 0.0 copy-done.3
  51.1 0.4 convert_reduce_fusion
  51.5 6.7 %multiply_bitcast_fusion = f32[4,128,4096]{2,1,0:T(8,128)} fusion(bf16[1,4,128,4096]{3,2,1,0:T(8,128)(2,1)} %param.10, f32[4]{0:T(128)S(1)} %compare_convert_fusion, f32[128,128]{1,0:T(8,128)S(1)} %get-tuple-element.29), kind=kOutput, calls=%fused_computation.5 | convolution fusion | flops 539000832 | bytes 12648464 | tf_op jit(solution)/shard_map/nk,tkd->tnd/dot_general | solution.py:61
  58.2 0.0 reduce-scatter.2.cloned.1.call-update
  58.2 81.5 %reduce-scatter.2.cloned.1.call-done = f32[1,128,4096]{2,1,0:T(8,128)} async-done(((f32[4,128,4096]{2,1,0:T(8,128)}), f32[1,128,4096]{2,1,0:T(8,128)}) %reduce-scatter.2.cloned.1.call-update) | async-done | bytes 2097168 | tf_op jit(solution)/shard_map/reduce_scatter | solution.py:64
  139.8 3.4 transpose_reshape.3
  143.2 0.0 copy-start.1
  143.2 0.0 copy-start.2
  143.2 59.8 %all_to_all.26 = f32[64,1,2,4096]{3,2,1,0:T(2,128)} all-to-all(f32[64,1,2,4096]{3,2,1,0:T(2,128)} %bitcast.79), channel_id=1, replica_groups=mesh['layer'=4,'latent'=64] {'latent'}, dimensions={0} | all-to-all | bytes 4194304 | tf_op jit(solution)/shard_map/all_to_all | solution.py:44
  203.0 2.2 reduce_sum.63
  205.3 0.0 copy-done.1
  205.3 0.0 copy-done.2
  205.3 0.1 fusion.25
  205.4 1.0 broadcast_in_dim.41
  206.4 33.9 %all_to_all.27 = bf16[64,1,2,4096]{3,2,1,0:T(2,128)(2,1)S(1)} all-to-all(bf16[64,1,2,4096]{3,2,1,0:T(2,128)(2,1)S(1)} %broadcast_in_dim.41), channel_id=1, replica_groups=mesh['layer'=4,'latent'=64] {'latent'}, dimensions={0} | all-to-all | bytes 2097152 | tf_op jit(solution)/shard_map/all_to_all | solution.py:22
  240.3 2.0 broadcast_in_dim.46
  242.3 7.6 %all-to-all-start.4 = ((f32[64,1,4096]{2,1,0:T(1,128)}), f32[64,1,4096]{2,1,0:T(1,128)}, u32[]{:S(2)}, u32[]{:S(2)}) async-start(f32[64,1,4096]{2,1,0:T(1,128)} %broadcast_in_dim.46), calls=%async_computation.5 | async-start | bytes 2097152 | tf_op jit(solution)/shard_map/all_to_all | solution.py:22
  249.8 1.2 stack_reshape_transpose.2
  251.0 1.6 copy.43
  252.7 23.9 %all-to-all-done.4 = f32[64,1,4096]{2,1,0:T(1,128)} async-done(((f32[64,1,4096]{2,1,0:T(1,128)}), f32[64,1,4096]{2,1,0:T(1,128)}, u32[]{:S(2)}, u32[]{:S(2)}) %all-to-all-start.4) | async-done | bytes 1048608 | tf_op jit(solution)/shard_map/all_to_all | solution.py:22
  276.5 2.5 stack.3
  279.0 7.8 %all-to-all-start.3 = ((bf16[4,1,128,4096]{2,3,1,0:T(8,128)(2,1)}), bf16[4,1,128,4096]{2,3,1,0:T(8,128)(2,1)}, u32[]{:S(2)}, u32[]{:S(2)}) async-start(bf16[4,1,128,4096]{2,3,1,0:T(8,128)(2,1)} %stack.3), calls=%async_computation.4 | async-start | bytes 8388608 | tf_op jit(solution)/shard_map/all_to_all | solution.py:13
  286.8 6.3 %copy.40 = bf16[1,4,128,4096]{2,3,1,0:T(8,128)(2,1)} copy(bf16[1,4,128,4096]{3,2,1,0:T(8,128)(2,1)} %param.10) | data formatting | bytes 8388608 | tf_op args[4]
  293.1 3.0 fusion
  296.1 0.1 multiply_reduce_fusion
  296.2 0.1 broadcast_multiply_fusion
  296.3 2.7 reduce_sum.69
  299.0 36.6 %all-to-all-done.3 = bf16[4,1,128,4096]{2,3,1,0:T(8,128)(2,1)} async-done(((bf16[4,1,128,4096]{2,3,1,0:T(8,128)(2,1)}), bf16[4,1,128,4096]{2,3,1,0:T(8,128)(2,1)}, u32[]{:S(2)}, u32[]{:S(2)}) %all-to-all-start.3) | async-done | bytes 4194336 | tf_op jit(solution)/shard_map/all_to_all | solution.py:13
  335.6 5.5 %fusion.29 = (f32[128]{0:T(128)}, bf16[128,128]{1,0:T(8,128)(2,1)S(1)}) fusion(f32[128,128]{1,0:T(8,128)S(1)} %get-tuple-element.29, f32[128]{0:T(128)S(1)} %get-tuple-element.27, bf16[1,4,128,4096]{3,2,1,0:T(8,128)(2,1)} %param.10, bf16[4,1,128,4096]{2,3,1,0:T(8,128)(2,1)} %all-to-all-done.3, pred[4]{0:T(512)(128)(4,1)S(1)} %broadcast_compare_fusion), kind=kOutput, calls=%fused_computation.36 | convolution fusion | flops 539049856 | bytes 8487940 | tf_op jit(solution)/shard_map/tnd,tkd->nk/dot_general | solution.py:75
  341.1 0.5 fusion.4
  341.5 1.3 copy.47
  342.8 6.8 %fusion.3 = bf16[1,4,128,4096]{2,3,1,0:T(8,128)(2,1)} fusion(bf16[1,4,128,4096]{2,3,1,0:T(8,128)(2,1)} %copy.40, f32[4,128]{1,0:T(4,128)S(1)} %broadcast_multiply_fusion, bf16[4,1,128,4096]{2,3,1,0:T(8,128)(2,1)} %all-to-all-done.3, pred[4]{0:T(512)(128)(4,1)S(1)} %broadcast_compare_fusion, f32[128,128]{1,0:T(8,128)S(1)} %get-tuple-element.29), kind=kOutput, calls=%fused_computation.6 | convolution fusion | flops 547389440 | bytes 12650500 | tf_op jit(solution)/shard_map/nk,tnd->tkd/dot_general | solution.py:85
  349.7 6.3 %copy.48 = bf16[1,4,128,4096]{3,2,1,0:T(8,128)(2,1)} copy(bf16[1,4,128,4096]{2,3,1,0:T(8,128)(2,1)} %fusion.3) | data formatting | bytes 8388608
  (3 shorter events, 0.0 us)
Async XLA Ops:
  7.2 43.9 %copy-start = (bf16[1,4096,128]{2,1,0:T(8,128)(2,1)S(1)}, bf16[1,4096,128]{2,1,0:T(8,128)(2,1)}, u32[]{:S(2)}) copy-start(bf16[1,4096,128]{2,1,0:T(8,128)(2,1)} %param.8) | copy-start | bytes 3145732
  7.2 43.9 %copy-start.3 = (f32[1,128]{1,0:T(1,128)S(1)}, f32[1,128]{1,0:T(1,128)}, u32[]{:S(2)}) copy-start(f32[1,128]{1,0:T(1,128)} %param.9) | copy-start | bytes 1540
  10.0 40.7 %all-to-all-start = ((bf16[64,2,4096]{2,1,0:T(2,128)(2,1)}), bf16[64,2,4096]{2,1,0:T(2,128)(2,1)S(1)}, u32[]{:S(2)}, u32[]{:S(2)}) async-start(bf16[64,2,4096]{2,1,0:T(2,128)(2,1)} %broadcast_in_dim.40), calls=%async_computation | async-start | bytes 2097152 | tf_op jit(solution)/shard_map/all_to_all | solution.py:22
  23.5 116.3 %reduce-scatter.2.cloned.1.call-start = ((), (), s32[]{:S(2)}) async-start(), calls=%async_computation.6 | async-start | bytes 10485760 | tf_op jit(solution)/shard_map/reduce_scatter | solution.py:64
  143.2 62.1 %copy-start.1 = (bf16[1,2,4096]{2,1,0:T(2,128)(2,1)S(1)}, bf16[1,2,4096]{2,1,0:T(2,128)(2,1)}, u32[]{:S(2)}) copy-start(bf16[1,2,4096]{2,1,0:T(2,128)(2,1)} %param.7) | copy-start | bytes 49156
  143.2 62.1 %copy-start.2 = (f32[1,4096]{1,0:T(1,128)S(1)}, f32[1,4096]{1,0:T(1,128)}, u32[]{:S(2)}) copy-start(f32[1,4096]{1,0:T(1,128)} %param.11) | copy-start | bytes 49156
  242.3 34.3 %all-to-all-start.4 = ((f32[64,1,4096]{2,1,0:T(1,128)}), f32[64,1,4096]{2,1,0:T(1,128)}, u32[]{:S(2)}, u32[]{:S(2)}) async-start(f32[64,1,4096]{2,1,0:T(1,128)} %broadcast_in_dim.46), calls=%async_computation.5 | async-start | bytes 2097152 | tf_op jit(solution)/shard_map/all_to_all | solution.py:22
  279.0 56.5 %all-to-all-start.3 = ((bf16[4,1,128,4096]{2,3,1,0:T(8,128)(2,1)}), bf16[4,1,128,4096]{2,3,1,0:T(8,128)(2,1)}, u32[]{:S(2)}, u32[]{:S(2)}) async-start(bf16[4,1,128,4096]{2,3,1,0:T(8,128)(2,1)} %stack.3), calls=%async_computation.4 | async-start | bytes 8388608 | tf_op jit(solution)/shard_map/all_to_all | solution.py:13
Sparse Core Ops, SparseCore 0:
  58.3 81.3 reduce-scatter.1
